TPU v7x, 128 devices: a whole 4x4x4 slice. The times are simulated.
128 devices in a mesh: rows: 32 (over z, x, core), width: 4 (over y).
Axes of the slice: x: 4, y: 4, z: 4, core: 2. Of those that a mesh axis runs over, the one named last changes fastest.
Arguments:
- weight_gate: float32 [2560, 9728], P('rows', 'width'), may hold values from -0.21875 to 0.21875
- moment_gate: float32 [2560, 9728], P('rows', 'width'), may hold values from -6 to 6
- square_gate: float32 [2560, 9728], P('rows', 'width'), may hold values from 0.1 to 10
- weight_up: float32 [2560, 9728], P('rows', 'width'), may hold values from -0.21875 to 0.21875
- moment_up: float32 [2560, 9728], P('rows', 'width'), may hold values from -6 to 6
- square_up: float32 [2560, 9728], P('rows', 'width'), may hold values from 0.1 to 10
- norm_gain: float32 [2560], P('rows'), may hold values from 0.25 to 1.75
Outputs:
- ready_gate: bfloat16 [2560, 9728], P(None, 'width')
- ready_up: bfloat16 [2560, 9728], P(None, 'width')
- column_gate: float32 [9728], P('width')
- column_up: float32 [9728], P('width')
All inputs are finite; a program needn't handle non-finite values.
Results may differ from a plain program's by a relative error of at most 0.0004.
Values may be sent and summed in bfloat16 or wider, within the bound.
A program may use at most 128 MiB of HBM per device.

v0:
```python
import jax
import jax.numpy as jnp
from jax import lax
from jax.sharding import PartitionSpec as P

learn_rate = 0.02
decay_rate = 0.1
tiny_value = 1e-08


def copy_for_each(array, axis):
    peers = lax.axis_size(axis)
    return lax.all_to_all(
        jnp.broadcast_to(array[None], (peers, *array.shape)), axis, 0, 0, tiled=True
    )


def taken_together(array, axis):
    everything = copy_for_each(array, axis)
    return jnp.sum(everything, axis=0)


def in_one(arrays, axis):
    line, at, gathered = (jnp.concatenate([a.reshape(-1) for a in arrays]), 0, [])
    so_far = taken_together(line, axis)
    for a in arrays:
        gathered.append(so_far[at : at + a.size].reshape(a.shape))
        at += a.size
    return tuple(gathered)


def side_by_side(arrays, axis, dim, along):
    ends, at = ([], 0)
    for a in arrays[:-1]:
        at += a.shape[along]
        ends.append(at)
    both = jnp.concatenate(arrays, axis=along)
    return tuple(jnp.split(lax.all_gather(both, axis, axis=dim, tiled=True), ends, axis=along))


def per_device(weight_gate, moment_gate, square_gate, weight_up, moment_up, square_up, norm_gain):
    latest_gate = weight_gate - learn_rate * (
        moment_gate / (jnp.sqrt(square_gate) + tiny_value) + decay_rate * weight_gate
    )
    latest_up = weight_up - learn_rate * (
        moment_up / (jnp.sqrt(square_up) + tiny_value) + decay_rate * weight_up
    )
    latest_gained_gate = latest_gate * norm_gain[:, None]
    latest_gained_up = latest_up * norm_gain[:, None]
    total_gate, total_up = in_one(
        (
            jnp.sum(latest_gained_gate * latest_gained_gate, axis=0),
            jnp.sum(latest_gained_up * latest_gained_up, axis=0),
        ),
        "rows",
    )
    column_gate = jnp.sqrt(total_gate)
    column_up = jnp.sqrt(total_up)
    narrow_gate, narrow_up = (
        (latest_gained_gate / column_gate).astype(jnp.bfloat16),
        (latest_gained_up / column_up).astype(jnp.bfloat16),
    )
    ready_gate, ready_up = side_by_side((narrow_gate, narrow_up), "rows", 0, 1)
    return (ready_gate, ready_up, column_gate, column_up)


def solution(mesh):
    in_specs = (
        P("rows", "width"),
        P("rows", "width"),
        P("rows", "width"),
        P("rows", "width"),
        P("rows", "width"),
        P("rows", "width"),
        P("rows"),
    )
    out_specs = (P(None, "width"), P(None, "width"), P("width"), P("width"))
    return jax.shard_map(
        per_device, mesh=mesh, in_specs=in_specs, out_specs=out_specs, check_vma=False
    )
```

profile of v0, /device:TPU:1, one launch (start us, length us, event | category | flops | bytes accessed | tf_op | source)
XLA Modules:
  0.0 147.5 jit_solution(14500008999192444338)
XLA Ops:
  7.2 0.0 all-gather.2.cloned.1.call-start
  7.2 3.2 %multiply_reduce_fusion.1 = (f32[2432]{0:T(1024)S(1)}, f32[80,2432]{1,0:T(8,128)S(1)}, f32[2432]{0:T(1024)S(1)}, f32[80,2432]{1,0:T(8,128)S(1)}) fusion(f32[80]{0:T(128)} %param.13, f32[80,2432]{1,0:T(8,128)} %param.7, f32[80,2432]{1,0:T(8,128)} %param.8, f32[80,2432]{1,0:T(8,128)} %param.9, f32[80,2432]{1,0:T(8,128)} %param.10, f32[80,2432]{1,0:T(8,128)} %param.11, ...), kind=kLoop, calls=%fused_computation.5 | loop fusion | flops 3497216 | bytes 6245696 | tf_op jit(solution)/shard_map/reduce_sum | solution.py:52
  10.5 0.3 broadcast_in_dim.2
  10.8 21.7 %all_to_all.6 = f32[32,1,4864]{2,1,0:T(1,128)S(1)} all-to-all(f32[32,1,4864]{2,1,0:T(1,128)S(1)} %broadcast_in_dim.2), channel_id=1, replica_groups=mesh['rows'=32,'width'=4] {'rows'}, dimensions={0} | all-to-all | bytes 1245184 | tf_op jit(solution)/shard_map/all_to_all | solution.py:13
  32.5 0.4 reduce_sum.29
  32.9 0.0 copy-start
  32.9 0.0 copy-start.1
  32.9 0.1 divide_convert_fusion
  33.0 0.9 pad_maximum_fusion
  34.0 0.0 all-gather.2.cloned.1.call-update
  34.0 89.6 %all-gather.2.cloned.1.call-done = bf16[2560,4864]{1,0:T(8,128)(2,1)} async-done(((bf16[80,4864]{1,0:T(8,128)(2,1)}), bf16[2560,4864]{1,0:T(8,128)(2,1)}) %all-gather.2.cloned.1.call-update) | async-done | bytes 24903696 | tf_op jit(solution)/shard_map/all_gather | solution.py:38
  123.6 17.0 %fusion = (bf16[2560,2432]{1,0:T(8,128)(2,1)}, bf16[2560,2432]{1,0:T(8,128)(2,1)}) fusion(bf16[2560,4864]{1,0:T(8,128)(2,1)} %all-gather.2.cloned.1.call-done), kind=kLoop, calls=%fused_computation.10 | loop fusion | bytes 49807360 | tf_op jit(solution)/shard_map/split | solution.py:38
  140.6 0.0 copy-done
  140.6 0.0 copy-done.1
  (2 shorter events, 0.0 us)
Async XLA Ops:
  7.2 116.4 %all-gather.2.cloned.1.call-start = ((), (), s32[]{:S(2)}) async-start(), calls=%async_computation.1 | async-start | bytes 25681920 | tf_op jit(solution)/shard_map/all_gather | solution.py:38
  32.9 107.7 %copy-start = (f32[2432]{0:T(1024)}, f32[2432]{0:T(1024)S(1)}, u32[]{:S(2)}) copy-start(f32[2432]{0:T(1024)S(1)} %get-tuple-element.10) | copy-start | bytes 29188
  32.9 107.7 %copy-start.1 = (f32[2432]{0:T(1024)}, f32[2432]{0:T(1024)S(1)}, u32[]{:S(2)}) copy-start(f32[2432]{0:T(1024)S(1)} %get-tuple-element.11) | copy-start | bytes 29188
Sparse Core Ops, SparseCore 0:
  34.1 89.4 all-gather.1
where the time goes:
time: 148 us; the launch traced here: 147 us
  waiting for transfers between devices  89.6 us (61%)
  blocking collectives  21.7 us (15%)
  local copies, waits for them, and re-layouts  17.4 us (12%)
  between operations  14.1 us (10%)
  other arithmetic  4.67 us (3%)
    all_gather x1, waiting for transfers between devices, side_by_side(): lax.all_gather(both, axis, axis=dim, tiled=True)  89.6 us
    all_to_all x1, blocking collectives, copy_for_each(): lax.all_to_all(jnp.broadcast_to(array[None], (peers, *array.shape)), axis...  21.7 us
    split x1, local copies, waits for them, and re-layouts, side_by_side(): jnp.split(lax.all_gather(both, axis, axis=dim, tiled=True), ends, axis=al...  17 us
    reduce_sum x1, other arithmetic, per_device(): jnp.sum(latest_gained_gate * latest_gained_gate, axis=0)  3.23 us
  transfers between devices with their start and end apart: 1, of which 1 were waited for; matrix products, arithmetic and copies ran while one was open for 0% of the time, Pallas kernels for 0%

commit v1 on v0

v1 whole, which is shorter than its diff:
```python
import jax
import jax.numpy as jnp
from jax import lax
from jax.experimental import pallas as pl
from jax.experimental.pallas import tpu as pltpu
from jax.sharding import PartitionSpec as P

MESH = pl.DeviceIdType.MESH

learn_rate = 0.02
decay_rate = 0.1
tiny_value = 1e-08

SIDE = 4
ROWS = 80
WIDE = 2432
TILES = WIDE // 128
HALVES = ((0, 1280), (1280, 1152))
GATE, UP = 0, 1

ORDER = (
    ("first", 0, False, 0),
    ("first", 0, False, 1),
    ("then", 0, False, 0),
    ("first", 0, True, None),
    ("then", 0, False, 1),
    ("then", -1, False, 0),
    ("then", 1, False, 0),
    ("then", -1, False, 1),
    ("then", 1, False, 1),
    ("then", 0, True, None),
    ("then", 2, False, 0),
    ("then", 2, False, 1),
    ("then", -1, True, None),
    ("then", 1, True, None),
    ("then", 2, True, None),
)
STEPS = len(ORDER)
LAG = 2
LINKS = (("x", 1), ("z", 1), ("x", -1), ("z", -1))
FLIP = {0: 0, -1: 1, 1: 0, 2: 1}


def item_of(axis, s, step):
    which, other, forwarded, half = ORDER[step]
    array = (GATE if axis == "x" else UP) if which == "first" else (UP if axis == "x" else GATE)
    if half is None:
        flip = 0 if which == "first" else FLIP[other]
        half = flip if s == 1 else 1 - flip
    along = -s if forwarded else 0
    return array, ((other, along) if axis == "x" else (along, other)), half


def arrival_of(array, offset, half):
    for link, (axis, s) in enumerate(LINKS):
        for step in range(STEPS):
            a, (dz, dx), h = item_of(axis, s, step)
            dz, dx = (dz, dx - s) if axis == "x" else (dz - s, dx)
            if a == array and h == half and (dz - offset[0]) % SIDE == 0 and (dx - offset[1]) % SIDE == 0:
                return link, step
    raise ValueError("no arrival")


def gather_kernel(
    wg, mg, sg, wu, mu, su, gain,
    out_g, out_u, col,
    held, latest, part, peer, xsum, zsum,
    in_sem, red_send, red_recv, ici_send, ici_recv, d2d_send, d2d_recv,
):
    me = lax.axis_index("rows")
    core = lax.rem(me, 2)
    chip = me // 2
    x = lax.rem(chip, SIDE)
    z = chip // SIDE
    outs = (out_g, out_u)

    def at(dz, dx):
        return (lax.rem(z + dz + 2 * SIDE, SIDE) * SIDE + lax.rem(x + dx + 2 * SIDE, SIDE)) * 2 + core

    sibling = chip * 2 + 1 - core

    loads = []
    for i, ref in enumerate((wg, mg, sg, wu, mu, su)):
        load = pltpu.make_async_copy(ref, held.at[i], in_sem.at[i])
        load.start()
        loads.append(load)

    barrier = pltpu.get_barrier_semaphore()
    greeted = [sibling] + [at(0, d) for d in (1, 2, 3)] + [at(d, 0) for d in (1, 2, 3)]
    for device in greeted:
        pl.semaphore_signal(barrier, inc=1, device_id={"rows": device}, device_id_type=MESH)

    def remote(src, dst, send, recv, device):
        copy = pltpu.make_async_remote_copy(
            src_ref=src, dst_ref=dst, send_sem=send, recv_sem=recv,
            device_id={"rows": device}, device_id_type=MESH,
        )
        return copy

    line = jnp.broadcast_to(gain[...], (ROWS, ROWS))
    here = lax.broadcasted_iota(jnp.int32, (ROWS, ROWS), 0) == lax.broadcasted_iota(jnp.int32, (ROWS, ROWS), 1)
    rows_gain = jnp.sum(jnp.where(here, line, 0.0), axis=1, keepdims=True)

    for a in (GATE, UP):
        for load in loads[3 * a : 3 * a + 3]:
            load.wait()

        def adam(j, _, a=a):
            tile = pl.ds(pl.multiple_of(j * 128, 128), 128)
            w = held[3 * a, :, tile]
            value = w - learn_rate * (
                held[3 * a + 1, :, tile] / (jnp.sqrt(held[3 * a + 2, :, tile]) + tiny_value) + decay_rate * w
            )
            value = value * rows_gain
            latest[a, :, tile] = value
            part[a, :, tile] = jnp.sum(value * value, axis=0, keepdims=True)
            return 0

        lax.fori_loop(0, TILES, adam, 0)

    pl.semaphore_wait(barrier, len(greeted))

    copies = [remote(part.at[1 - core], peer, red_send.at[0], red_recv.at[0], sibling)]
    copies[0].start()
    copies[0].wait_recv()
    xsum[x] = part[core] + peer[...]
    for d in (1, 2, 3):
        copy = remote(xsum.at[x], xsum.at[x], red_send.at[d], red_recv.at[d], at(0, d))
        copy.start()
        copies.append(copy)
    for copy in copies[1:4]:
        copy.wait_recv()
    zsum[z] = xsum[0] + xsum[1] + xsum[2] + xsum[3]
    for d in (1, 2, 3):
        copy = remote(zsum.at[z], zsum.at[z], red_send.at[3 + d], red_recv.at[3 + d], at(d, 0))
        copy.start()
        copies.append(copy)
    for copy in copies[4:7]:
        copy.wait_recv()
    col[core] = jnp.sqrt(zsum[0] + zsum[1] + zsum[2] + zsum[3])
    copy = remote(col.at[core], col.at[core], red_send.at[7], red_recv.at[7], sibling)
    copy.start()
    copies.append(copy)
    copy.wait_recv()

    mine = pl.ds(pl.multiple_of(me * ROWS, 16), ROWS)
    for a in (GATE, UP):

        def scale(j, _, a=a):
            tile = pl.ds(pl.multiple_of(j * 128, 128), 128)
            inverse = 1.0 / col[a, :, tile]
            outs[a][mine, tile] = (latest[a, :, tile] * inverse).astype(jnp.bfloat16)
            return 0

        lax.fori_loop(0, TILES, scale, 0)

    def rows_of(offset):
        return pl.ds(pl.multiple_of(at(*offset) * ROWS, 16), ROWS)

    def piece(array, offset, half):
        return outs[array].at[rows_of(offset), pl.ds(*HALVES[half])]

    sent = [[None] * STEPS for _ in LINKS]
    arrived = set()
    passed = []

    def pass_on(src, slot):
        copy = remote(src, src, d2d_send.at[slot], d2d_recv.at[slot], sibling)
        copy.start()
        passed.append(copy)

    def arrive(link, step):
        if (link, step) in arrived:
            return
        arrived.add((link, step))
        axis, s = LINKS[link]
        array, (dz, dx), half = item_of(axis, s, step)
        offset = (dz, dx - s) if axis == "x" else (dz - s, dx)
        landed = piece(array, offset, half)
        pltpu.make_async_copy(landed, landed, ici_recv.at[link * STEPS + step]).wait()
        pass_on(landed, 2 + link * STEPS + step)

    for step in range(STEPS):
        for link, (axis, s) in enumerate(LINKS):
            array, offset, half = item_of(axis, s, step)
            if offset != (0, 0):
                arrive(*arrival_of(array, offset, half))
            src = piece(array, offset, half)
            slot = link * STEPS + step
            target = at(0, s) if axis == "x" else at(s, 0)
            copy = remote(src, src, ici_send.at[slot], ici_recv.at[slot], target)
            copy.start()
            sent[link][step] = copy
        if step == 0:
            for a in (GATE, UP):
                pass_on(outs[a].at[mine], a)
        if step >= LAG:
            for link in range(len(LINKS)):
                arrive(link, step - LAG)
    for step in range(STEPS - LAG, STEPS):
        for link in range(len(LINKS)):
            arrive(link, step)

    for copy in copies:
        copy.wait_send()
    for line_of in sent:
        for copy in line_of:
            copy.wait_send()
    for copy in passed:
        copy.wait_send()
    theirs = at(0, 0) + 1 - 2 * core
    for a in (GATE, UP):
        landed = outs[a].at[pl.ds(pl.multiple_of(theirs * ROWS, 16), ROWS)]
        pltpu.make_async_copy(landed, landed, d2d_recv.at[a]).wait()
    for link, (axis, s) in enumerate(LINKS):
        for step in range(STEPS):
            array, (dz, dx), half = item_of(axis, s, step)
            offset = (dz, dx - s) if axis == "x" else (dz - s, dx)
            row = at(*offset) + 1 - 2 * core
            landed = outs[array].at[pl.ds(pl.multiple_of(row * ROWS, 16), ROWS), pl.ds(*HALVES[half])]
            pltpu.make_async_copy(landed, landed, d2d_recv.at[2 + link * STEPS + step]).wait()


def gather(*args):
    hbm = pl.BlockSpec(memory_space=pltpu.HBM)
    vmem = pl.BlockSpec(memory_space=pltpu.VMEM)
    whole = SIDE * SIDE * 2 * ROWS
    return pl.pallas_call(
        gather_kernel,
        out_shape=(
            pltpu.VMEM((whole, WIDE), jnp.bfloat16),
            pltpu.VMEM((whole, WIDE), jnp.bfloat16),
            pltpu.VMEM((2, 1, WIDE), jnp.float32),
        ),
        in_specs=[hbm] * 6 + [vmem],
        out_specs=(vmem, vmem, vmem),
        scratch_shapes=[
            pltpu.VMEM((6, ROWS, WIDE), jnp.float32),
            pltpu.VMEM((2, ROWS, WIDE), jnp.float32),
            pltpu.VMEM((2, 1, WIDE), jnp.float32),
            pltpu.VMEM((1, WIDE), jnp.float32),
            pltpu.VMEM((SIDE, 1, WIDE), jnp.float32),
            pltpu.VMEM((SIDE, 1, WIDE), jnp.float32),
            pltpu.SemaphoreType.DMA((6,)),
            pltpu.SemaphoreType.DMA((8,)),
            pltpu.SemaphoreType.DMA((8,)),
            pltpu.SemaphoreType.DMA((4 * STEPS,)),
            pltpu.SemaphoreType.DMA((4 * STEPS,)),
            pltpu.SemaphoreType.DMA((2 + 4 * STEPS,)),
            pltpu.SemaphoreType.DMA((2 + 4 * STEPS,)),
        ],
        compiler_params=pltpu.CompilerParams(
            collective_id=0, has_side_effects=True, vmem_limit_bytes=36 * 2**20
        ),
        name="gather",
    )(*args)


PIECES = 8


def put_kernel(g, u, col, ready_g, ready_u, column_g, column_u, sem):
    copies = []
    for a, (src, dst) in enumerate(((g, ready_g), (u, ready_u))):
        rows = src.shape[0] // PIECES
        for i in range(PIECES):
            part = pl.ds(i * rows, rows)
            copy = pltpu.make_async_copy(src.at[part], dst.at[part], sem.at[a * PIECES + i])
            copy.start()
            copies.append(copy)
    column_g[...] = col[GATE, 0, :]
    column_u[...] = col[UP, 0, :]
    for copy in copies:
        copy.wait()


def put(g, u, col):
    hbm = pl.BlockSpec(memory_space=pl.ANY)
    vmem = pl.BlockSpec(memory_space=pltpu.VMEM)
    return pl.pallas_call(
        put_kernel,
        out_shape=(
            jax.ShapeDtypeStruct(g.shape, g.dtype),
            jax.ShapeDtypeStruct(u.shape, u.dtype),
            jax.ShapeDtypeStruct((WIDE,), jnp.float32),
            jax.ShapeDtypeStruct((WIDE,), jnp.float32),
        ),
        in_specs=[hbm, hbm, vmem],
        out_specs=(hbm, hbm, vmem, vmem),
        scratch_shapes=[pltpu.SemaphoreType.DMA((2 * PIECES,))],
        compiler_params=pltpu.CompilerParams(vmem_limit_bytes=2**20),
        name="put",
    )(g, u, col)


def per_device(weight_gate, moment_gate, square_gate, weight_up, moment_up, square_up, norm_gain):
    weights = (weight_gate, moment_gate, square_gate, weight_up, moment_up, square_up)
    weights = [pltpu.with_memory_space_constraint(a, pltpu.HBM) for a in weights]
    g, u, col = gather(*weights, norm_gain.reshape(1, ROWS))
    return put(g, u, col)


def solution(mesh):
    in_specs = (P("rows", "width"),) * 6 + (P("rows"),)
    out_specs = (P(None, "width"), P(None, "width"), P("width"), P("width"))
    return jax.shard_map(
        per_device, mesh=mesh, in_specs=in_specs, out_specs=out_specs, check_vma=False
    )
```

time: 148 us -> 95.7 us (0.65)
  Pallas kernels: 0 us -> 95 us
  waiting for transfers between devices: 89.6 us -> 0 us
  blocking collectives: 21.7 us -> 0 us
  local copies, waits for them, and re-layouts: 17.4 us -> 0 us
  between operations: 14.1 us -> 0.64 us
  other arithmetic: 4.67 us -> 0 us
    pallas_call x0 -> x2, Pallas kernels: none -> 95 us  [the longest x1 85.9 us: gather(): pl.pallas_call(gather_kernel, out_shape=(pltpu.VMEM((whole, WIDE), jnp.bf...]
    all_gather x1 -> x0, waiting for transfers between devices: 89.6 us -> none  [side_by_side(): lax.all_gather(both, axis, axis=dim, tiled=True)]
    all_to_all x1 -> x0, blocking collectives: 21.7 us -> none  [copy_for_each(): lax.all_to_all(jnp.broadcast_to(array[None], (peers, *array.shape)), axis...]
    split x1 -> x0, local copies, waits for them, and re-layouts: 17 us -> none  [side_by_side(): jnp.split(lax.all_gather(both, axis, axis=dim, tiled=True), ends, axis=al...]
    reduce_sum x2 -> x0, other arithmetic: 3.59 us -> none  [the longest x1 3.23 us: per_device(): jnp.sum(latest_gained_gate * latest_gained_gate, axis=0)]
  transfers between devices with their start and end apart: 1 -> 0, of which waited for: 1 -> 0; matrix products, arithmetic and copies ran while one was open for 0% -> 0% of each run, Pallas kernels for 0% -> 0%
where the time goes in v1:
time: 95.7 us; the launch traced here: 95.6 us
  Pallas kernels  95 us (99%)
    pallas_call x1, Pallas kernels, gather(): pl.pallas_call(gather_kernel, out_shape=(pltpu.VMEM((whole, WIDE), jnp.bf...  85.9 us
    pallas_call x1, Pallas kernels, put(): pl.pallas_call(put_kernel, out_shape=(jax.ShapeDtypeStruct(g.shape, g.dty...  9.04 us

profile of v1, /device:TPU:1, one launch (start us, length us, event | category | flops | bytes accessed | tf_op | source)
XLA Modules:
  0.0 95.6 jit_solution(7517067398766405198)
XLA Ops:
  0.6 85.9 %gather.1 = (bf16[2560,2432]{1,0:T(8,128)(2,1)S(1)}, bf16[2560,2432]{1,0:T(8,128)(2,1)S(1)}, f32[2,1,2432]{2,1,0:T(1,128)S(1)}) custom-call(f32[80,2432]{1,0:T(8,128)} %wg.1, f32[80,2432]{1,0:T(8,128)} %mg.1, f32[80,2432]{1,0:T(8,128)} %sg.1, f32[80,2432]{1,0:T(8,128)} %wu.1, f32[80,2432]{1,0:T(8,128)} %mu.1, f32[80,2432]{1,0:T(8,128)} %su.1, f32[1,80]{1,0:T(1,128)} %bitcast.1), custom_call_target="tpu_custom_call" | custom-call | tf_op jit(solution)/shard_map/gather/pallas_call | solution.py:228
  86.6 9.0 %put.1 = (bf16[2560,2432]{1,0:T(8,128)(2,1)}, bf16[2560,2432]{1,0:T(8,128)(2,1)}, f32[2432]{0:T(1024)}, f32[2432]{0:T(1024)}) custom-call(bf16[2560,2432]{1,0:T(8,128)(2,1)S(1)} %get-tuple-element.7.g, bf16[2560,2432]{1,0:T(8,128)(2,1)S(1)} %get-tuple-element.8.u, f32[2,1,2432]{2,1,0:T(1,128)S(1)} %get-tuple-element.9.col), custom_call_target="tpu_custom_call" | custom-call | tf_op jit(solution)/shard_map/put/pallas_call | solution.py:280
